TPU v7x, 32 devices: a whole 2x2x4 slice. The times are simulated.
32 devices in a mesh: row: 4 (over x, core), col: 8 (over z, y).
Axes of the slice: x: 2, y: 2, z: 4, core: 2. Of those that a mesh axis runs over, the one named last changes fastest.
Arguments:
- normed: bfloat16 [12288, 6144], P(('row', 'col')), may hold values from -6 to 6
- out_grad: bfloat16 [12288, 6144], P(('row', 'col')), may hold values from -0.125 to 0.125
- w_in: bfloat16 [6144, 48], replicated, may hold values from -0.078125 to 0.078125
- hidden_grad: bfloat16 [12288, 48], P(('row', 'col')), may hold values from -0.125 to 0.125
- qkv_grad: bfloat16 [12288, 64], P(('row', 'col')), may hold values from -0.125 to 0.125
- bucket_order: int32 [160], replicated, may hold values from 0 to 159, each once
Outputs:
- buckets: bfloat16 [160, 6144], replicated
Inputs may be any that keep to these rules, and one draw needn't show every extreme that they name: bucket_order is a permutation of 0 to 159.
All inputs are finite; a program needn't handle non-finite values.
Results may differ from a plain program's by a relative error of at most 0.0044.
Values may be sent and summed in bfloat16 or wider, within the bound.
A program may use at most 64 MiB of HBM per device.

v0:
```python
import jax
import jax.numpy as jnp
from jax import lax
from jax.sharding import PartitionSpec as P

NB = 4


def local(normed, out_grad, w_in, hidden_grad, qkv_grad, bucket_order):
    pre = jnp.dot(normed, w_in, preferred_element_type=jnp.float32)
    cdf = 0.5 * (1.0 + lax.erf(pre * 0.7071067811865476))
    pdf = jnp.exp(-0.5 * pre * pre) * 0.3989422804014327
    hidden = (pre * cdf).astype(jnp.bfloat16)
    pre_grad = (hidden_grad.astype(jnp.float32) * (cdf + pre * pdf)).astype(jnp.bfloat16)
    grad_qkv = jnp.dot(qkv_grad.T, normed, preferred_element_type=jnp.float32)
    grad_in = jnp.dot(pre_grad.T, normed, preferred_element_type=jnp.float32)
    grad_out = jnp.dot(hidden.T, out_grad, preferred_element_type=jnp.float32)
    stacked = jnp.concatenate([grad_qkv, grad_in, grad_out], axis=0)
    ordered = jnp.take(stacked, bucket_order, axis=0)
    per_bucket = ordered.shape[0] // NB
    results = []
    for bucket in range(NB):
        piece = ordered[bucket * per_bucket : (bucket + 1) * per_bucket]
        summed = lax.psum(piece, ("row", "col")).astype(jnp.bfloat16)
        results.append(summed)
    return jnp.concatenate(results, axis=0)


def solution(mesh):
    in_specs = (
        P(("row", "col"), None),
        P(("row", "col"), None),
        P(),
        P(("row", "col"), None),
        P(("row", "col"), None),
        P(),
    )
    out_specs = P()
    return jax.shard_map(local, mesh=mesh, in_specs=in_specs, out_specs=out_specs, check_vma=False)
```

profile of v0, /device:TPU:0, one launch (start us, length us, event | category | flops | bytes accessed | tf_op | source)
XLA Modules:
  0.0 118.2 jit_solution(10145399101433720630)
XLA Ops:
  0.0 0.0 copy-start
  0.0 0.0 copy-start.2
  0.0 1.1 copy-done
  1.1 4.3 %fusion.15 = f32[384,48]{0,1:T(8,128)S(1)} fusion(bf16[384,6144]{1,0:T(8,128)(2,1)} %param.6, bf16[6144,48]{0,1:T(8,128)(2,1)S(1)} %copy-done), kind=kOutput, calls=%fused_computation.24 | convolution fusion | flops 226492416 | bytes 5382144 | tf_op jit(solution)/shard_map/dot_general | solution.py:10
  5.4 0.0 copy-done.2
  5.4 0.0 copy-start.1
  5.4 0.0 copy-start.4
  5.4 0.9 fusion.6
  6.4 1.4 %copy-done.1 = bf16[384,6144]{1,0:T(8,128)(2,1)S(1)} copy-done((bf16[384,6144]{1,0:T(8,128)(2,1)S(1)}, bf16[384,6144]{1,0:T(8,128)(2,1)}, u32[]{:S(2)}) %copy-start.1) | copy-done | bytes 4718616
  7.7 0.0 copy-done.4
  7.7 0.0 copy-start.3
  7.7 0.9 fusion.7
  8.7 0.0 copy-done.3
  8.7 0.9 fusion.14
  9.6 0.0 copy-start.5
  9.7 2.1 %pad_maximum_fusion = f32[160,6144]{1,0:T(8,128)} fusion(f32[48,6144]{1,0:T(8,128)S(1)} %fusion.6, f32[48,6144]{1,0:T(8,128)S(1)} %fusion.7, f32[64,6144]{1,0:T(8,128)S(1)} %fusion.14), kind=kLoop, calls=%fused_computation.1 | loop fusion | flops 1966080 | bytes 7864320 | tf_op jit(solution)/shard_map/concatenate | solution.py:18
  11.8 0.0 copy-done.5
  11.8 7.4 %gather_fusion = f32[160,6144]{1,0:T(8,128)} fusion(f32[160,6144]{1,0:T(8,128)} %pad_maximum_fusion, s32[1024]{0:T(1024)S(1)} %pad_clamp_fusion), kind=kCustom, calls=%fused_computation | custom fusion | bytes 7864960 | tf_op jit(solution)/shard_map/jit(_take)/gather | solution.py:19
  19.3 2.7 %broadcast_select_fusion = f32[160,6144]{1,0:T(8,128)S(1)} fusion(f32[160,6144]{1,0:T(8,128)} %gather_fusion, pred[160]{0:T(512)(128)(4,1)S(1)} %compare_and_fusion), kind=kLoop, calls=%fused_computation.3 | loop fusion | flops 983040 | bytes 7864480 | tf_op jit(solution)/shard_map/jit(_take)/select_n | solution.py:19
  22.0 1.2 %fusion.13 = (f32[40,6144]{1,0:T(8,128)S(1)}, f32[40,6144]{1,0:T(8,128)S(1)}, f32[40,6144]{1,0:T(8,128)S(1)}, f32[40,6144]{1,0:T(8,128)}) fusion(f32[160,6144]{1,0:T(8,128)S(1)} %broadcast_select_fusion), kind=kLoop, calls=%fused_computation.22 | loop fusion | bytes 7864320 | tf_op jit(solution)/shard_map/slice | solution.py:23
  23.2 92.1 %all-reduce.2 = (bf16[40,6144]{1,0:T(8,128)(2,1)}, bf16[40,6144]{1,0:T(8,128)(2,1)}, bf16[40,6144]{1,0:T(8,128)(2,1)}, bf16[40,6144]{1,0:T(8,128)(2,1)}) all-reduce(f32[40,6144]{1,0:T(8,128)S(1)} %get-tuple-element.10, f32[40,6144]{1,0:T(8,128)S(1)} %get-tuple-element.11, ...), channel_id=1, replica_groups=mesh['row'=4,'col'=8] {'row','col'}, use_global_device_ids=true, to_apply=%region_3.4 | all-reduce | flops 983040 | bytes 5898240 | tf_op jit(solution)/shard_map/psum | solution.py:24
  115.3 2.9 %pad_maximum_fusion.1 = bf16[160,6144]{1,0:T(8,128)(2,1)} fusion(bf16[40,6144]{1,0:T(8,128)(2,1)} %get-tuple-element.5, bf16[40,6144]{1,0:T(8,128)(2,1)} %get-tuple-element.6, bf16[40,6144]{1,0:T(8,128)(2,1)} %get-tuple-element.7, bf16[40,6144]{1,0:T(8,128)(2,1)} %get-tuple-element.8), kind=kLoop, calls=%fused_computation.2 | loop fusion | flops 7864320 | bytes 3932160 | tf_op jit(solution)/shard_map/concatenate | solution.py:26
  (3 shorter events, 0.0 us)
Async XLA Ops:
  0.0 1.1 copy-start
  0.0 5.4 %copy-start.2 = (bf16[384,6144]{1,0:T(8,128)(2,1)S(1)}, bf16[384,6144]{1,0:T(8,128)(2,1)}, u32[]{:S(2)}) copy-start(bf16[384,6144]{1,0:T(8,128)(2,1)} %param.7) | copy-start | bytes 14155780
  5.4 2.3 %copy-start.1 = (bf16[384,6144]{1,0:T(8,128)(2,1)S(1)}, bf16[384,6144]{1,0:T(8,128)(2,1)}, u32[]{:S(2)}) copy-start(bf16[384,6144]{1,0:T(8,128)(2,1)} %param.6) | copy-start | bytes 14155780
  5.4 2.3 %copy-start.4 = (bf16[384,48]{0,1:T(8,128)(2,1)S(1)}, bf16[384,48]{0,1:T(8,128)(2,1)}, u32[]{:S(2)}) copy-start(bf16[384,48]{0,1:T(8,128)(2,1)} %param.9) | copy-start | bytes 110596
  7.7 0.9 copy-start.3
  9.6 2.2 %copy-start.5 = (s32[160]{0:T(256)S(1)}, s32[160]{0:T(256)}, u32[]{:S(2)}) copy-start(s32[160]{0:T(256)} %param.11) | copy-start | bytes 1924
where the time goes:
time: 118 us
  blocking collectives  92.1 us (78%)
  local copies, waits for them, and re-layouts  11.1 us (9%)
  other arithmetic  7.78 us (7%)
  matrix products  7.13 us (6%)
    psum x1, blocking collectives, local(): summed = lax.psum(piece, ('row', 'col')).astype(jnp.bfloat16)  92.1 us
    gather x1, local copies, waits for them, and re-layouts, local(): ordered = jnp.take(stacked, bucket_order, axis=0)  7.44 us
    dot_general x1, matrix products, local(): pre = jnp.dot(normed, w_in, preferred_element_type=jnp.float32)  4.31 us
    concatenate x1, other arithmetic, local(): return jnp.concatenate(results, axis=0)  2.92 us
    select_n x2, other arithmetic, local(): ordered = jnp.take(stacked, bucket_order, axis=0)  2.7 us
    unnamed x12, local copies, waits for them, and re-layouts  2.46 us

commit v1 on v0

--- a/solution.py
+++ b/solution.py
@@ -21,7 +21,7 @@
     results = []
     for bucket in range(NB):
         piece = ordered[bucket * per_bucket : (bucket + 1) * per_bucket]
-        summed = lax.psum(piece, ("row", "col")).astype(jnp.bfloat16)
+        summed = lax.psum(lax.psum(piece, "col"), "row").astype(jnp.bfloat16)
         results.append(summed)
     return jnp.concatenate(results, axis=0)
 

time: 118 us -> 264 us (2.24)
  waiting for transfers between devices: 0 us -> 152 us
  blocking collectives: 92.1 us -> 72.4 us
  between operations: 0.08 us -> 13.5 us
    psum x0 -> x1, waiting for transfers between devices: none -> 152 us  [local(): summed = lax.psum(lax.psum(piece, 'col'), 'row').astype(jnp.bfloat16)]
    psum x1, blocking collectives: 92.1 us -> 72.4 us  [local(): summed = lax.psum(lax.psum(piece, 'col'), 'row').astype(jnp.bfloat16)]
  transfers between devices with their start and end apart: 0 -> 1, of which waited for: 0 -> 1; matrix products, arithmetic and copies ran while one was open for 0% -> 0% of each run, Pallas kernels for 0% -> 0%
where the time goes in v1:
time: 264 us
  waiting for transfers between devices  152 us (58%)
  blocking collectives  72.4 us (27%)
  between operations  13.5 us (5%)
  local copies, waits for them, and re-layouts  10.8 us (4%)
  other arithmetic  8.19 us (3%)
  matrix products  6.64 us (3%)
    psum x1, waiting for transfers between devices, local(): summed = lax.psum(lax.psum(piece, 'col'), 'row').astype(jnp.bfloat16)  152 us
    psum x1, blocking collectives, local(): summed = lax.psum(lax.psum(piece, 'col'), 'row').astype(jnp.bfloat16)  72.4 us
    gather x1, local copies, waits for them, and re-layouts, local(): ordered = jnp.take(stacked, bucket_order, axis=0)  7.44 us
  transfers between devices with their start and end apart: 1, of which 1 were waited for; matrix products, arithmetic and copies ran while one was open for 0% of the time, Pallas kernels for 0%

profile of v1, /device:TPU:0, one launch (start us, length us, event | category | flops | bytes accessed | tf_op | source)
XLA Modules:
  0.0 264.0 jit_solution(742018976522438746)
XLA Ops:
  6.5 0.0 copy-start
  6.5 0.0 all-reduce.5.cloned.1.call-start
  6.5 0.0 copy-start.2
  6.5 0.8 compare_select_fusion
  7.4 1.1 compare_and_fusion
  8.5 0.0 copy-done
  8.5 3.8 %fusion.15 = f32[384,48]{0,1:T(8,128)S(1)} fusion(bf16[384,6144]{1,0:T(8,128)(2,1)} %param.6, bf16[6144,48]{0,1:T(8,128)(2,1)S(1)} %copy-done), kind=kOutput, calls=%fused_computation.24 | convolution fusion | flops 226492416 | bytes 5382144 | tf_op jit(solution)/shard_map/dot_general | solution.py:10
  12.3 0.0 copy-done.2
  12.3 0.0 copy-start.1
  12.3 0.0 copy-start.4
  12.3 0.9 fusion.6
  13.3 1.4 copy-done.1
  14.6 0.0 copy-done.4
  14.6 0.0 copy-start.3
  14.6 0.9 fusion.7
  15.6 0.0 copy-done.3
  15.6 0.9 fusion.14
  16.6 2.2 pad_maximum_fusion
  18.7 7.4 %gather_fusion = f32[160,6144]{1,0:T(8,128)} fusion(f32[160,6144]{1,0:T(8,128)} %pad_maximum_fusion, s32[1024]{0:T(1024)S(1)} %pad_clamp_fusion), kind=kCustom, calls=%fused_computation | custom fusion | bytes 7864960 | tf_op jit(solution)/shard_map/jit(_take)/gather | solution.py:19
  26.2 2.7 %broadcast_select_fusion = f32[160,6144]{1,0:T(8,128)S(1)} fusion(f32[160,6144]{1,0:T(8,128)} %gather_fusion, pred[160]{0:T(512)(128)(4,1)S(1)} %compare_and_fusion), kind=kLoop, calls=%fused_computation.3 | loop fusion | flops 983040 | bytes 7864480 | tf_op jit(solution)/shard_map/jit(_take)/select_n | solution.py:19
  28.9 2.0 fusion.13
  30.9 0.0 all-reduce.5.cloned.1.call-update
  30.9 152.4 %all-reduce.5.cloned.1.call-done = (f32[40,6144]{1,0:T(8,128)}, f32[40,6144]{1,0:T(8,128)}, f32[40,6144]{1,0:T(8,128)}, f32[40,6144]{1,0:T(8,128)}) async-done(((f32[40,6144]{1,0:T(8,128)}, f32[40,6144]{1,0:T(8,128)}, f32[40,6144]{1,0:T(8,128)}, f32[40,6144]{1,0:T(8,128)}), (f32[40,6144]{1,0:T(8,128)}, f32[40,6144]{1,0:T(8,128)}, f32[40,6144]{1,0:T(8,128)}, ...) | async-done | bytes 3932176 | tf_op jit(solution)/shard_map/psum | solution.py:24
  183.3 72.4 %all-reduce.6 = (bf16[40,6144]{1,0:T(8,128)(2,1)S(1)}, bf16[40,6144]{1,0:T(8,128)(2,1)S(1)}, bf16[40,6144]{1,0:T(8,128)(2,1)S(1)}, bf16[40,6144]{1,0:T(8,128)(2,1)S(1)}) all-reduce(f32[40,6144]{1,0:T(8,128)} %get-tuple-element.5, f32[40,6144]{1,0:T(8,128)} %get-tuple-element.6, ...), channel_id=1, replica_groups=mesh['row'=4,'col'=8] {'row'}, use_global_device_ids=true, to_apply=%region_7.8 | all-reduce | flops 983040 | bytes 5898240 | tf_op jit(solution)/shard_map/psum | solution.py:24
  255.7 1.4 pad_maximum_fusion.1
  (1 shorter events, 0.0 us)
Async XLA Ops:
  6.5 1.9 copy-start
  6.5 176.8 %all-reduce.5.cloned.1.call-start = ((), (), s32[]{:S(2)}) async-start(), calls=%async_computation | async-start | bytes 7864320 | tf_op jit(solution)/shard_map/psum | solution.py:24
  6.5 5.8 %copy-start.2 = (bf16[384,6144]{1,0:T(8,128)(2,1)S(1)}, bf16[384,6144]{1,0:T(8,128)(2,1)}, u32[]{:S(2)}) copy-start(bf16[384,6144]{1,0:T(8,128)(2,1)} %param.7) | copy-start | bytes 14155780
  12.3 2.3 copy-start.1
  12.3 2.3 copy-start.4
  14.6 0.9 copy-start.3
Sparse Core Ops, SparseCore 0:
  31.0 152.2 all-reduce.4
